TPU v7x, 32 devices: a whole 2x2x4 slice. The times are simulated.
32 devices in a mesh: row: 4 (over x, core), col: 2 (over y), depth: 4 (over z).
Axes of the slice: x: 2, y: 2, z: 4, core: 2. Of those that a mesh axis runs over, the one named last changes fastest.
Arguments:
- diag_two: float32 [256, 256], replicated, may hold values from -3 to 3, as said below
- diag_one: float32 [256, 256], replicated, may hold values from -3 to 3, as said below
- cross_tile: float32 [256, 256], replicated, may hold values from -0.375 to 0.375
- left_two: float32 [256, 4096], P(None, ('col', 'depth')), may hold values from -0.375 to 0.375
- left_one: float32 [256, 4096], P(None, ('col', 'depth')), may hold values from -0.375 to 0.375
- below_left: float32 [4096, 4096], P('row', ('col', 'depth')), may hold values from -0.09375 to 0.09375
- panel_two: float32 [4096, 256], P('row', 'col'), may hold values from -0.09375 to 0.09375
- panel_one: float32 [4096, 256], P('row', 'col'), may hold values from -0.09375 to 0.09375
- grad_diag_two: float32 [256, 256], replicated, may hold values from -6 to 6
- grad_diag_one: float32 [256, 256], replicated, may hold values from -6 to 6
- grad_cross: float32 [256, 256], replicated, may hold values from -6 to 6
- grad_left_two: float32 [256, 4096], P('row', ('col', 'depth')), may hold values from -6 to 6
- grad_left_one: float32 [256, 4096], P('row', ('col', 'depth')), may hold values from -6 to 6
- grad_below: float32 [4096, 4096], P('row', ('col', 'depth')), may hold values from -6 to 6
- grad_panel_two: float32 [4096, 256], P('row', 'col'), may hold values from -6 to 6
- grad_panel_one: float32 [4096, 256], P('row', 'col'), may hold values from -6 to 6
Outputs:
- out_below: float32 [4096, 4096], P('row', ('col', 'depth'))
- out_left_two: float32 [256, 4096], P('row', ('col', 'depth'))
- out_left_one: float32 [256, 4096], P('row', ('col', 'depth'))
- out_diag_two: float32 [256, 256], replicated
- out_diag_one: float32 [256, 256], replicated
- out_cross: float32 [256, 256], replicated
- out_panel_two: float32 [4096, 256], P('row', 'col')
- out_panel_one: float32 [4096, 256], P('row', 'col')
Inputs may be any that keep to these rules, and one draw needn't show every extreme that they name: `diag_two`: lower triangular; its diagonal lies in 1 to 3. `diag_one`: lower triangular; its diagonal lies in 1 to 3.
All inputs are finite; a program needn't handle non-finite values.
Results may differ from a plain program's by a relative error of at most 0.000071.
Values sent between devices are 32-bit elements; how exact they have to be, the bound alone decides.
A program may use at most 64 MiB of HBM per device.

v0:
```python
import jax
import jax.numpy as jnp
from jax import lax
from jax.sharding import PartitionSpec as P


def matmul(left, right):
    return jnp.dot(left, right, precision=lax.Precision.HIGHEST, preferred_element_type=jnp.float32)


def right_solve(factor, values):
    return lax.linalg.triangular_solve(factor, values, left_side=False, lower=True)


def halved(square):
    return jnp.tril(square) - 0.5 * jnp.diag(jnp.diag(square))


def reverse_block(factor, cotangent):
    inner = halved(matmul(factor.T, cotangent))
    leftward = lax.linalg.triangular_solve(
        factor, inner, left_side=True, lower=True, transpose_a=True
    )
    spread = right_solve(factor, leftward)
    return spread + spread.T


def body(
    diag_two,
    diag_one,
    cross_tile,
    left_two,
    left_one,
    below_left,
    panel_two,
    panel_one,
    grad_diag_two,
    grad_diag_one,
    grad_cross,
    grad_left_two,
    grad_left_one,
    grad_below,
    grad_panel_two,
    grad_panel_one,
):
    share = grad_left_two.shape[0]
    width = panel_two.shape[1]
    row_start = lax.axis_index("row") * share
    col_start = lax.axis_index("col") * width
    grad_two_all, panel_two_all, grad_one_all, panel_one_all = (
        lax.all_gather(grad_panel_two, "col", axis=1, tiled=True),
        lax.all_gather(panel_two, "col", axis=1, tiled=True),
        lax.all_gather(grad_panel_one, "col", axis=1, tiled=True),
        lax.all_gather(panel_one, "col", axis=1, tiled=True),
    )
    solved_two = right_solve(diag_two, grad_two_all)
    gram_two, gram_cross = lax.psum(
        (matmul(solved_two.T, panel_two_all), matmul(solved_two.T, panel_one_all)), "row"
    )
    below_first = grad_below - matmul(solved_two, left_two)
    sym_two = reverse_block(diag_two, grad_diag_two - jnp.tril(gram_two))
    cross_next = grad_cross - gram_cross - matmul(sym_two, cross_tile)
    out_cross = right_solve(diag_one, cross_next)
    panel_next = grad_one_all - matmul(solved_two, cross_tile)
    out_panel_one = right_solve(diag_one, panel_next)
    gram_below = lax.psum(matmul(out_panel_one.T, panel_one_all), "row")
    summed_both = lax.psum_scatter(
        jnp.concatenate(
            [matmul(solved_two.T, below_left), matmul(out_panel_one.T, below_left)], axis=1
        ),
        "row",
        scatter_dimension=0,
        tiled=True,
    )
    summed_two = summed_both[:, : left_two.shape[1]]
    summed_one = summed_both[:, left_two.shape[1] :]
    out_below = below_first - matmul(out_panel_one, left_one)
    gram_one = matmul(out_cross.T, cross_tile) + gram_below
    sym_one = reverse_block(diag_one, grad_diag_one - jnp.tril(gram_one))
    sym_two_rows = lax.dynamic_slice_in_dim(sym_two, row_start, share, 0)
    sym_one_rows = lax.dynamic_slice_in_dim(sym_one, row_start, share, 0)
    cross_rows = lax.dynamic_slice_in_dim(out_cross, row_start, share, 0)
    cross_cols = lax.dynamic_slice_in_dim(out_cross, row_start, share, 1)
    out_left_two = (
        grad_left_two - summed_two - matmul(sym_two_rows, left_two) - matmul(cross_rows, left_one)
    )
    out_left_one = (
        grad_left_one - matmul(cross_cols.T, left_two) - summed_one - matmul(sym_one_rows, left_one)
    )
    out_panel_two = lax.dynamic_slice_in_dim(solved_two, col_start, width, 1)
    panel_one_cols = lax.dynamic_slice_in_dim(out_panel_one, col_start, width, 1)
    return (
        out_below,
        out_left_two,
        out_left_one,
        halved(sym_two),
        halved(sym_one),
        out_cross,
        out_panel_two,
        panel_one_cols,
    )


def solution(mesh):
    return jax.shard_map(
        body,
        mesh=mesh,
        in_specs=(
            P(),
            P(),
            P(),
            P(None, ("col", "depth")),
            P(None, ("col", "depth")),
            P("row", ("col", "depth")),
            P("row", "col"),
            P("row", "col"),
            P(),
            P(),
            P(),
            P("row", ("col", "depth")),
            P("row", ("col", "depth")),
            P("row", ("col", "depth")),
            P("row", "col"),
            P("row", "col"),
        ),
        out_specs=(
            P("row", ("col", "depth")),
            P("row", ("col", "depth")),
            P("row", ("col", "depth")),
            P(),
            P(),
            P(),
            P("row", "col"),
            P("row", "col"),
        ),
        check_vma=False,
    )
```

profile of v0, /device:TPU:0, one launch (start us, length us, event | category | flops | bytes accessed | tf_op | source)
XLA Modules:
  0.0 185.2 jit_solution(10981025533135270904)
XLA Ops:
  10.2 4.0 %while.14 = (s32[]{:T(128)}, f32[256,256]{1,0:T(8,128)S(1)}, s32[2,2]{1,0:T(2,128)S(1)}, f32[2,128,128]{2,1,0:T(8,128)S(1)}, s32[]{:T(128)}) while((s32[]{:T(128)}, f32[256,256]{1,0:T(8,128)S(1)}, s32[2,2]{1,0:T(2,128)S(1)}, f32[2,128,128]{2,1,0:T(8,128)S(1)}, s32[]{:T(128)}) %tuple.61), condition=%wide.while_cond, body=%wide.while_body.sunk | while | flops 2 | bytes 131181 | solution.py:12
  14.2 19.7 %custom-call.21 = f32[2,128,128]{1,2,0:T(8,128)S(1)} custom-call(f32[2,128,128]{2,1,0:T(8,128)S(1)} %get-tuple-element.59), custom_call_target="InvertDiagBlocksLowerTriangular" | custom-call | tf_op jit(solution)/shard_map/triangular_solve/custom-call.1 | solution.py:12
  34.0 4.0 %while.15 = (s32[]{:T(128)}, f32[256,256]{1,0:T(8,128)S(1)}, s32[2,2]{1,0:T(2,128)S(1)}, f32[2,128,128]{2,1,0:T(8,128)S(1)}, s32[]{:T(128)}) while((s32[]{:T(128)}, f32[256,256]{1,0:T(8,128)S(1)}, s32[2,2]{1,0:T(2,128)S(1)}, f32[2,128,128]{2,1,0:T(8,128)S(1)}, s32[]{:T(128)}) %tuple.80), condition=%wide.while_cond.clone, body=%wide.while_body.clone.sunk | while | flops 2 | bytes 131181 | solution.py:12
  38.0 19.9 %custom-call.22 = f32[2,128,128]{1,2,0:T(8,128)S(1)} custom-call(f32[2,128,128]{2,1,0:T(8,128)S(1)} %get-tuple-element.60), custom_call_target="InvertDiagBlocksLowerTriangular" | custom-call | tf_op jit(solution)/shard_map/triangular_solve/custom-call.1 | solution.py:12
  58.7 1.8 copy.41
  62.2 2.0 %convolution_subtract_fusion.2 = f32[1024,128]{1,0:T(8,128)S(1)} fusion(f32[128,1024]{1,0:T(8,128)S(1)} %fusion.9, f32[1024,256]{1,0:T(8,128)} %all-gather.5.cloned.1.call-done, f32[256,256]{1,0:T(8,128)S(1)} %get-tuple-element.210), kind=kOutput, calls=%fused_computation.17 | convolution fusion | flops 201457664 | bytes 1638400 | tf_op jit(solution)/shard_map/triangular_solve/dot.4 | solution.py:12
  65.7 3.2 %convolution_subtract_fusion = f32[1024,256]{1,0:T(8,128)S(1)} fusion(f32[1024,256]{1,0:T(8,128)} %all-gather.7.cloned.1.call-done, f32[256,256]{1,0:T(8,128)} %param.24, f32[1024,128]{0,1:T(8,128)S(1)} %bitcast.117, f32[1024,128]{0,1:T(8,128)S(1)} %fusion.40), kind=kOutput, calls=%fused_computation.9 | convolution fusion | flops 805830656 | bytes 3407872 | tf_op jit(solution)/shard_map/dot_general | solution.py:8
  73.2 2.0 %copy.48 = f32[1024,128]{1,0:T(8,128)} copy(f32[1024,128]{0,1:T(8,128)} %get-tuple-element.106) | data formatting | bytes 1048576
  75.2 2.0 %copy.49 = f32[1024,128]{1,0:T(8,128)} copy(f32[1024,128]{0,1:T(8,128)} %get-tuple-element.105) | data formatting | bytes 1048576
  77.3 2.4 %all-gather.11.cloned.1.call-done = f32[1024,256]{1,0:T(8,128)} async-done(((f32[1024,128]{1,0:T(8,128)}), f32[1024,256]{1,0:T(8,128)}) %all-gather.11.cloned.1.call-update) | async-done | bytes 1048592 | tf_op jit(solution)/shard_map/all_gather | solution.py:54
  79.7 4.2 %fusion.3 = f32[256,256]{0,1:T(8,128)} fusion(f32[1024,256]{1,0:T(8,128)} %all-gather.11.cloned.1.call-done, f32[1024,128]{0,1:T(8,128)} %bitcast.124, f32[1024,128]{0,1:T(8,128)} %copy-done.3), kind=kOutput, calls=%fused_computation.35 | convolution fusion | flops 805568512 | bytes 2359296 | tf_op jit(solution)/shard_map/dot_general | solution.py:8
  85.6 2.7 %fusion.4 = f32[256,512]{1,0:T(8,128)} fusion(f32[1024,512]{1,0:T(8,128)S(1)} %copy-done, f32[1024,128]{0,1:T(8,128)S(1)} %bitcast.126, f32[1024,128]{0,1:T(8,128)S(1)} %copy-done.4), kind=kOutput, calls=%fused_computation.36 | convolution fusion | flops 1610874880 | bytes 3670016 | tf_op jit(solution)/shard_map/dot_general | solution.py:8
  88.4 3.0 %fusion.13 = f32[256,512]{1,0:T(8,128)} fusion(f32[1024,512]{1,0:T(8,128)S(1)} %copy-done, f32[1024,128]{0,1:T(8,128)S(1)} %bitcast.120, f32[1024,128]{0,1:T(8,128)S(1)} %fusion.40), kind=kOutput, calls=%fused_computation.50 | convolution fusion | flops 1610874880 | bytes 3670016 | tf_op jit(solution)/shard_map/dot_general | solution.py:8
  91.4 11.0 %all-gather.9.cloned.1.call-done = f32[1024,256]{1,0:T(8,128)} async-done(((f32[1024,128]{1,0:T(8,128)}), f32[1024,256]{1,0:T(8,128)}) %all-gather.9.cloned.1.call-update) | async-done | bytes 1048592 | tf_op jit(solution)/shard_map/all_gather | solution.py:52
  102.3 3.7 %fusion.12 = f32[256,256]{0,1:T(8,128)} fusion(f32[1024,256]{1,0:T(8,128)} %all-gather.9.cloned.1.call-done, f32[1024,128]{0,1:T(8,128)S(1)} %bitcast.121, f32[1024,128]{0,1:T(8,128)S(1)} %fusion.40), kind=kOutput, calls=%fused_computation.49 | convolution fusion | flops 805568512 | bytes 2359296 | tf_op jit(solution)/shard_map/dot_general | solution.py:8
  106.2 2.3 %pad_maximum_fusion.2 = f32[256,1024]{1,0:T(8,128)} fusion(f32[256,512]{1,0:T(8,128)} %fusion.4, f32[256,512]{1,0:T(8,128)} %fusion.13), kind=kLoop, calls=%fused_computation.34 | loop fusion | flops 262144 | bytes 2097152 | tf_op jit(solution)/shard_map/concatenate | solution.py:68
  108.5 4.2 %fusion.14 = f32[1024,512]{1,0:T(8,128)} fusion(f32[256,512]{1,0:T(8,128)} %param.25, f32[1024,128]{0,1:T(8,128)S(1)} %bitcast.122, f32[1024,128]{0,1:T(8,128)S(1)} %fusion.40), kind=kOutput, calls=%fused_computation.51 | convolution fusion | flops 1610874880 | bytes 3670016 | tf_op jit(solution)/shard_map/dot_general | solution.py:8
  112.7 6.0 %subtract_subtract_fusion = f32[1024,512]{1,0:T(8,128)} fusion(f32[1024,512]{1,0:T(8,128)} %param.35, f32[1024,512]{1,0:T(8,128)} %fusion.14, f32[256,512]{1,0:T(8,128)} %param.26, f32[1024,128]{0,1:T(8,128)} %bitcast.125, f32[1024,128]{0,1:T(8,128)} %copy-done.3), kind=kOutput, calls=%fused_computation.8 | convolution fusion | flops 1611923456 | bytes 7864320 | tf_op jit(solution)/shard_map/dot_general | solution.py:8
  118.7 22.5 %all-reduce.3.cloned.1.call-done = (f32[256,256]{0,1:T(8,128)}, f32[256,256]{1,0:T(8,128)}, f32[256,256]{0,1:T(8,128)}) async-done(((f32[256,256]{0,1:T(8,128)}, f32[256,256]{1,0:T(8,128)}, f32[256,256]{0,1:T(8,128)}), (f32[256,256]{0,1:T(8,128)}, f32[256,256]{1,0:T(8,128)}, f32[256,256]{0,1:T(8,128)})) %all-reduce.3.cloned.1.call-update) | async-done | bytes 786448 | tf_op jit(solution)/shard_map/psum | solution.py:57
  142.6 2.6 %gather_fusion = f32[256]{0:T(256)S(1)} fusion(f32[256,256]{0,1:T(8,128)S(1)} %convolution_bitcast_fusion.1, s32[256]{0:T(256)S(1)} %bitcast.113), kind=kCustom, calls=%fused_computation | custom fusion | bytes 4096 | tf_op jit(solution)/shard_map/jit(_diag)/jit(diagonal)/cond/branch_0_fun/gather | solution.py:16
  149.1 2.4 %gather_fusion.2 = f32[256]{0:T(256)S(1)} fusion(f32[256,256]{0,1:T(8,128)S(1)} %bitcast_add_fusion.1, s32[256]{0:T(256)S(1)} %bitcast.114), kind=kCustom, calls=%fused_computation.2 | custom fusion | bytes 4096 | tf_op jit(solution)/shard_map/jit(_diag)/jit(diagonal)/cond/branch_0_fun/gather | solution.py:16
  156.2 2.4 %gather_fusion.1 = f32[256]{0:T(256)S(1)} fusion(f32[256,256]{0,1:T(8,128)S(1)} %convolution_bitcast_fusion, s32[256]{0:T(256)S(1)} %bitcast.115), kind=kCustom, calls=%fused_computation.1 | custom fusion | bytes 4096 | tf_op jit(solution)/shard_map/jit(_diag)/jit(diagonal)/cond/branch_0_fun/gather | solution.py:16
  165.7 2.4 %gather_fusion.3 = f32[256]{0:T(256)S(1)} fusion(f32[256,256]{0,1:T(8,128)S(1)} %bitcast_add_fusion, s32[256]{0:T(256)S(1)} %bitcast.116), kind=kCustom, calls=%fused_computation.3 | custom fusion | bytes 4096 | tf_op jit(solution)/shard_map/jit(_diag)/jit(diagonal)/cond/branch_0_fun/gather | solution.py:16
  174.6 2.2 %convolution_subtract_fusion.4 = f32[64,512]{1,0:T(8,128)} fusion(f32[64,512]{1,0:T(8,128)S(1)} %fusion.2, f32[256,512]{1,0:T(8,128)} %param.26, f32[256,256]{0,1:T(8,128)S(1)} %bitcast_add_fusion, s32[]{:T(128)S(6)} %select_n.58), kind=kOutput, calls=%fused_computation.24 | convolution fusion | flops 100696064 | bytes 917508 | tf_op jit(solution)/shard_map/dot_general | solution.py:8
  (138 shorter events, 45.6 us)
Async XLA Ops:
  7.2 78.5 %copy-start = (f32[1024,512]{1,0:T(8,128)S(1)}, f32[1024,512]{1,0:T(8,128)}, u32[]{:S(2)}) copy-start(f32[1024,512]{1,0:T(8,128)} %param.27) | copy-start | bytes 6291460
  7.2 26.7 %copy-start.18 = (f32[256,256]{1,0:T(8,128)S(1)}, f32[256,256]{1,0:T(8,128)}, u32[]{:S(2)}) copy-start(f32[256,256]{1,0:T(8,128)} %param.23) | copy-start | bytes 786436
  7.2 53.3 %all-gather.5.cloned.1.call-start = ((), (), s32[]{:S(2)}) async-start(), calls=%async_computation.1 | async-start | bytes 1572864 | tf_op jit(solution)/shard_map/all_gather | solution.py:51
  7.9 57.8 %all-gather.7.cloned.1.call-start = ((), (), s32[]{:S(2)}) async-start(), calls=%async_computation.2 | async-start | bytes 1572864 | tf_op jit(solution)/shard_map/all_gather | solution.py:53
  8.7 49.2 %copy-start.25 = (f32[256,256]{1,0:T(8,128)S(1)}, f32[256,256]{1,0:T(8,128)}, u32[]{:S(2)}) copy-start(f32[256,256]{1,0:T(8,128)} %param.30) | copy-start | bytes 786436
  8.7 71.0 %all-gather.11.cloned.1.call-start = ((), (), s32[]{:S(2)}) async-start(), calls=%async_computation.5 | async-start | bytes 1572864 | tf_op jit(solution)/shard_map/all_gather | solution.py:54
  9.4 92.9 %all-gather.9.cloned.1.call-start = ((), (), s32[]{:S(2)}) async-start(), calls=%async_computation.4 | async-start | bytes 1572864 | tf_op jit(solution)/shard_map/all_gather | solution.py:52
  10.0 131.2 %all-reduce.3.cloned.1.call-start = ((), (), s32[]{:S(2)}) async-start(), calls=%async_computation.6 | async-start | bytes 1572864 | tf_op jit(solution)/shard_map/psum | solution.py:57
  14.2 47.9 %copy-start.10 = (f32[256,256]{1,0:T(8,128)}, f32[256,256]{1,0:T(8,128)S(1)}, u32[]{:S(2)}) copy-start(f32[256,256]{1,0:T(8,128)S(1)} %get-tuple-element.210) | copy-start | bytes 786436
  33.9 28.2 %copy-start.15 = (f32[2,128,128]{1,2,0:T(8,128)}, f32[2,128,128]{1,2,0:T(8,128)S(1)}, u32[]{:S(2)}) copy-start(f32[2,128,128]{1,2,0:T(8,128)S(1)} %custom-call.21) | copy-start | bytes 393220
  38.0 115.5 %copy-start.8 = (f32[256,256]{1,0:T(8,128)}, f32[256,256]{1,0:T(8,128)S(1)}, u32[]{:S(2)}) copy-start(f32[256,256]{1,0:T(8,128)S(1)} %get-tuple-element.209) | copy-start | bytes 786436
  57.9 12.7 %copy-start.13 = (f32[2,128,128]{1,2,0:T(8,128)}, f32[2,128,128]{1,2,0:T(8,128)S(1)}, u32[]{:S(2)}) copy-start(f32[2,128,128]{1,2,0:T(8,128)S(1)} %custom-call.22) | copy-start | bytes 393220
  79.7 5.9 %copy-start.2 = (f32[128,1024]{1,0:T(8,128)S(1)}, f32[128,1024]{1,0:T(8,128)}, u32[]{:S(2)}) copy-start(f32[128,1024]{1,0:T(8,128)} %copy-done.1) | copy-start | bytes 1572868
  79.7 5.9 %copy-start.4 = (f32[1024,128]{0,1:T(8,128)S(1)}, f32[1024,128]{0,1:T(8,128)}, u32[]{:S(2)}) copy-start(f32[1024,128]{0,1:T(8,128)} %copy-done.3) | copy-start | bytes 1572868
  106.1 67.0 %reduce-scatter.2.cloned.1.call-start = ((), (), s32[]{:S(2)}) async-start(), calls=%async_computation.3 | async-start | bytes 1310720 | tf_op jit(solution)/shard_map/reduce_scatter | solution.py:67
  112.7 28.5 %copy-start.22 = (f32[256,256]{1,0:T(8,128)S(1)}, f32[256,256]{1,0:T(8,128)}, u32[]{:S(2)}) copy-start(f32[256,256]{1,0:T(8,128)} %param.22) | copy-start | bytes 786436
  112.7 28.5 %copy-start.23 = (f32[256,256]{0,1:T(8,128)S(1)}, f32[256,256]{0,1:T(8,128)}, u32[]{:S(2)}) copy-start(f32[256,256]{0,1:T(8,128)} %copy.37) | copy-start | bytes 786436
  118.7 26.5 %copy-start.16 = (f32[2,128,128]{1,2,0:T(8,128)S(1)}, f32[2,128,128]{1,2,0:T(8,128)}, u32[]{:S(2)}) copy-start(f32[2,128,128]{1,2,0:T(8,128)} %copy-done.15) | copy-start | bytes 393220
  118.7 26.8 %copy-start.11 = (f32[256,256]{1,0:T(8,128)S(1)}, f32[256,256]{1,0:T(8,128)}, u32[]{:S(2)}) copy-start(f32[256,256]{1,0:T(8,128)} %copy-done.10) | copy-start | bytes 786436
  146.5 5.0 %copy-start.12 = (f32[256,256]{1,0:T(8,128)S(1)}, f32[256,256]{1,0:T(8,128)}, u32[]{:S(2)}) copy-start(f32[256,256]{1,0:T(8,128)} %param.24) | copy-start | bytes 786436
  148.9 4.3 %copy-start.14 = (f32[2,128,128]{1,2,0:T(8,128)S(1)}, f32[2,128,128]{1,2,0:T(8,128)}, u32[]{:S(2)}) copy-start(f32[2,128,128]{1,2,0:T(8,128)} %copy-done.13) | copy-start | bytes 393220
  155.8 4.7 %copy-start.9 = (f32[256,256]{1,0:T(8,128)S(1)}, f32[256,256]{1,0:T(8,128)}, u32[]{:S(2)}) copy-start(f32[256,256]{1,0:T(8,128)} %copy-done.8) | copy-start | bytes 786436
  164.6 8.6 %copy-start.5 = (f32[256,512]{1,0:T(8,128)S(1)}, f32[256,512]{1,0:T(8,128)}, u32[]{:S(2)}) copy-start(f32[256,512]{1,0:T(8,128)} %param.25) | copy-start | bytes 1572868
  165.6 7.5 %copy-start.27 = (f32[64,512]{1,0:T(8,128)S(1)}, f32[64,512]{1,0:T(8,128)}, u32[]{:S(2)}) copy-start(f32[64,512]{1,0:T(8,128)} %param.34) | copy-start | bytes 393220
  (11 other events, 31.2 us)
Sparse Core Ops, SparseCore 0:
  9.5 24.0 all-gather.4
  35.2 21.4 all-gather.6
  58.2 21.4 all-gather.10
  81.1 21.2 all-gather.8
  106.2 34.9 all-reduce.2
  143.6 24.7 reduce-scatter.1
where the time goes:
time: 186 us; the launch traced here: 185 us
  matrix products  53.4 us (29%)
  other arithmetic  45.8 us (25%)
  waiting for transfers between devices  38.5 us (21%)
  local copies, waits for them, and re-layouts  32.2 us (17%)
  between operations  14.8 us (8%)
    another operation x9, other arithmetic, right_solve(): lax.linalg.triangular_solve(factor, values, left_side=False, lower=True)  40.8 us
    dot_general x16, matrix products, matmul(): jnp.dot(left, right, precision=lax.Precision.HIGHEST, preferred_element_t...  39 us
    psum x1, waiting for transfers between devices, body(): lax.psum((matmul(solved_two.T, panel_two_all), matmul(solved_two.T, panel...  22.5 us
    unnamed x65, local copies, waits for them, and re-layouts  13.4 us
    another operation x15, matrix products, right_solve(): lax.linalg.triangular_solve(factor, values, left_side=False, lower=True)  11.7 us
    all_gather x1, waiting for transfers between devices, body(): lax.all_gather(panel_two, 'col', axis=1, tiled=True)  11 us
    gather x4, local copies, waits for them, and re-layouts, halved(): return jnp.tril(square) - 0.5 * jnp.diag(jnp.diag(square))  9.74 us
    another operation x19, local copies, waits for them, and re-layouts, right_solve(): lax.linalg.triangular_solve(factor, values, left_side=False, lower=True)  9.13 us
  transfers between devices with their start and end apart: 6, of which 3 were waited for; matrix products, arithmetic and copies ran while one was open for 65% of the time, Pallas kernels for 0%

commit v1 on v0

v1 whole, which is shorter than its diff:
```python
import jax
import jax.numpy as jnp
from jax import lax
from jax.experimental import pallas as pl
from jax.experimental.pallas import tpu as pltpu
from jax.sharding import PartitionSpec as P


def large(left, right, contract):
    return lax.dot_general(
        left,
        right,
        ((contract[:1], contract[1:]), ((), ())),
        precision=lax.Precision.HIGH,
        preferred_element_type=jnp.float32,
    )


def small(left, right, contract=(1, 0)):
    return lax.dot_general(
        left,
        right,
        ((contract[:1], contract[1:]), ((), ())),
        precision=lax.Precision.HIGHEST,
        preferred_element_type=jnp.float32,
    )


def grid_of(size):
    rows = lax.broadcasted_iota(jnp.int32, (size, size), 0)
    cols = lax.broadcasted_iota(jnp.int32, (size, size), 1)
    return rows, cols


def invert_all(blocks):
    size = blocks[0].shape[0]
    rows, cols = grid_of(size)
    apart = rows ^ cols
    lower = rows > cols
    inverses = []
    for block in blocks:
        diagonal = jnp.where(rows == cols, block, 0.0)
        down = 1.0 / jnp.sum(diagonal, axis=1, keepdims=True)
        across = 1.0 / jnp.sum(diagonal, axis=0, keepdims=True)
        pair = jnp.where(lower & (apart == 1), block, 0.0)
        inverses.append(jnp.where(rows == cols, down, 0.0) - pair * down * across)
    level = 1
    while (2 << level) <= size:
        mask = lower & ((apart >> level) == 1)
        steps = [
            small(jnp.where(mask, block, 0.0), inverse) for block, inverse in zip(blocks, inverses)
        ]
        inverses = [inverse - small(inverse, step) for inverse, step in zip(inverses, steps)]
        level += 1
    return inverses


def invert_kernel(two_ref, one_ref, cross_ref, inv_two_ref, inv_one_ref, cross_inv_ref):
    half = two_ref.shape[0] // 2
    refs = (two_ref, one_ref)
    outs = (inv_two_ref, inv_one_ref)
    blocks = []
    for ref in refs:
        blocks += [ref[:half, :half], ref[half:, half:]]
    inverses = invert_all(blocks)
    steps = [small(ref[half:, :half], inverses[2 * at]) for at, ref in enumerate(refs)]
    for at, out in enumerate(outs):
        out[:half, :half] = inverses[2 * at]
        out[half:, half:] = inverses[2 * at + 1]
        out[:half, half:] = jnp.zeros((half, half), jnp.float32)
        out[half:, :half] = -small(inverses[2 * at + 1], steps[at])
    cross_inv_ref[...] = small(cross_ref[...], inv_one_ref[...])


def chain_kernel(
    two_ref,
    one_ref,
    cross_ref,
    inv_two_ref,
    inv_one_ref,
    grad_two_ref,
    grad_one_ref,
    grad_cross_ref,
    grams_ref,
    sym_two_ref,
    sym_one_ref,
    half_two_ref,
    half_one_ref,
    out_cross_ref,
):
    size = two_ref.shape[0]
    rows, cols = grid_of(size)
    lower = rows >= cols
    scale = jnp.where(rows > cols, 1.0, jnp.where(rows == cols, 0.5, 0.0))

    def sym(factor, inverse, cotangent):
        inner = scale * small(factor, cotangent, (0, 0))
        spread = small(small(inverse, inner, (0, 0)), inverse)
        return spread + spread.T

    gram_two = grams_ref[:size, :]
    gram_cross = grams_ref[size : 2 * size, :]
    gram_below = grams_ref[2 * size :, :]
    sym_two = sym(
        two_ref[...], inv_two_ref[...], grad_two_ref[...] - jnp.where(lower, gram_two, 0.0)
    )
    sym_two_ref[...] = sym_two
    half_two_ref[...] = scale * sym_two
    cross_next = grad_cross_ref[...] - gram_cross - small(sym_two, cross_ref[...])
    out_cross = small(cross_next, inv_one_ref[...])
    out_cross_ref[...] = out_cross
    gram_one = small(out_cross, cross_ref[...], (0, 0)) + gram_below
    sym_one = sym(
        one_ref[...], inv_one_ref[...], grad_one_ref[...] - jnp.where(lower, gram_one, 0.0)
    )
    sym_one_ref[...] = sym_one
    half_one_ref[...] = scale * sym_one


def local_call(kernel, operands, count, flops):
    size = operands[0].shape[0]
    moved = 4 * size * size * (len(operands) + count)
    return pl.pallas_call(
        kernel,
        out_shape=[jax.ShapeDtypeStruct((size, size), jnp.float32)] * count,
        in_specs=[pl.BlockSpec(memory_space=pltpu.VMEM)] * len(operands),
        out_specs=[pl.BlockSpec(memory_space=pltpu.VMEM)] * count,
        cost_estimate=pl.CostEstimate(flops=flops, bytes_accessed=moved, transcendentals=0),
    )(*operands)


def swap(values, axis, bit):
    size = lax.axis_size(axis)
    return lax.ppermute(values, axis, [(at, at ^ bit) for at in range(size)])


def gathered(values, axis):
    if lax.axis_size(axis) != 2:
        return [(lax.all_gather(values, axis, axis=1, tiled=True), 0)]
    width = values.shape[1]
    at = lax.axis_index(axis)
    return [(values, at * width), (swap(values, axis, 1), (1 - at) * width)]


def times(pieces, factor):
    total = None
    for values, start in pieces:
        rows = lax.dynamic_slice_in_dim(factor, start, values.shape[1], 0)
        part = large(values, rows, (1, 0))
        total = part if total is None else total + part
    return total


def assembled(values, axis):
    size = lax.axis_size(axis)
    if size != 2:
        return lax.all_gather(values, axis, axis=1, tiled=True)
    other = swap(values, axis, 1)
    first = lax.axis_index(axis) == 0
    return jnp.concatenate(
        [jnp.where(first, values, other), jnp.where(first, other, values)], axis=1
    )


def halve(values, axis, bit):
    mine = (lax.axis_index(axis) // bit) % 2
    keep = lax.dynamic_index_in_dim(values, mine, 0, keepdims=False)
    give = lax.dynamic_index_in_dim(values, 1 - mine, 0, keepdims=False)
    return keep + swap(give, axis, bit)


def scatter_sum(values, axis):
    size = lax.axis_size(axis)
    if size & (size - 1):
        return lax.psum_scatter(values, axis, scatter_dimension=0, tiled=False)
    bit = 1
    while bit < size:
        paired = values.reshape((-1, 2) + values.shape[1:])
        values = halve(jnp.moveaxis(paired, 1, 0), axis, bit)
        bit *= 2
    return values[0]


def row_sum(values, axis, columns):
    size = lax.axis_size(axis)
    if size & (size - 1) or size < 2:
        return assembled(lax.psum(values, axis), columns)
    part = halve(values.reshape((2, -1) + values.shape[1:]), axis, 1)
    bit = 2
    while bit < size:
        part = part + swap(part, axis, bit)
        bit *= 2
    part = assembled(part, columns)
    other = swap(part, axis, 1)
    even = lax.axis_index(axis) % 2 == 0
    return jnp.concatenate([jnp.where(even, part, other), jnp.where(even, other, part)], axis=0)


def body(
    diag_two,
    diag_one,
    cross_tile,
    left_two,
    left_one,
    below_left,
    panel_two,
    panel_one,
    grad_diag_two,
    grad_diag_one,
    grad_cross,
    grad_left_two,
    grad_left_one,
    grad_below,
    grad_panel_two,
    grad_panel_one,
):
    size = diag_two.shape[0]
    share = grad_left_two.shape[0]
    width = panel_two.shape[1]
    row_start = lax.axis_index("row") * share
    col_start = lax.axis_index("col") * width
    cube = 2 * size**3

    pieces_two = gathered(grad_panel_two, "col")
    pieces_one = gathered(grad_panel_one, "col")
    inv_two, inv_one, cross_inv = local_call(
        invert_kernel, (diag_two, diag_one, cross_tile), 3, 60 * cube
    )
    solved_two = times(pieces_two, inv_two)
    solved_one = times(pieces_one, inv_one) - large(solved_two, cross_inv, (1, 0))
    partial = jnp.concatenate(
        [
            large(solved_two, panel_two, (0, 0)),
            large(solved_two, panel_one, (0, 0)),
            large(solved_one, panel_one, (0, 0)),
        ],
        axis=0,
    )
    grams = row_sum(partial, "row", "col")
    rows = lax.axis_size("row")
    lefts = jnp.stack(
        [
            large(solved_two, below_left, (0, 0)).reshape(rows, share, -1),
            large(solved_one, below_left, (0, 0)).reshape(rows, share, -1),
        ],
        axis=1,
    )
    summed = scatter_sum(lefts, "row")
    out_below = (
        grad_below - large(solved_two, left_two, (1, 0)) - large(solved_one, left_one, (1, 0))
    )
    sym_two, sym_one, half_two, half_one, out_cross = local_call(
        chain_kernel,
        (
            diag_two,
            diag_one,
            cross_tile,
            inv_two,
            inv_one,
            grad_diag_two,
            grad_diag_one,
            grad_cross,
            grams,
        ),
        5,
        60 * cube,
    )
    sym_two_rows = lax.dynamic_slice_in_dim(sym_two, row_start, share, 0)
    sym_one_rows = lax.dynamic_slice_in_dim(sym_one, row_start, share, 0)
    cross_rows = lax.dynamic_slice_in_dim(out_cross, row_start, share, 0)
    cross_cols = lax.dynamic_slice_in_dim(out_cross, row_start, share, 1)
    out_left_two = (
        grad_left_two
        - summed[0]
        - large(sym_two_rows, left_two, (1, 0))
        - large(cross_rows, left_one, (1, 0))
    )
    out_left_one = (
        grad_left_one
        - summed[1]
        - large(cross_cols, left_two, (0, 0))
        - large(sym_one_rows, left_one, (1, 0))
    )
    return (
        out_below,
        out_left_two,
        out_left_one,
        half_two,
        half_one,
        out_cross,
        lax.dynamic_slice_in_dim(solved_two, col_start, width, 1),
        lax.dynamic_slice_in_dim(solved_one, col_start, width, 1),
    )


def solution(mesh):
    panels = P("row", "col")
    lefts = P(None, ("col", "depth"))
    blocks = P("row", ("col", "depth"))
    return jax.shard_map(
        body,
        mesh=mesh,
        in_specs=(P(), P(), P(), lefts, lefts, blocks, panels, panels)
        + (P(), P(), P(), blocks, blocks, blocks, panels, panels),
        out_specs=(blocks, blocks, blocks, P(), P(), P(), panels, panels),
        check_vma=False,
    )
```

time: 186 us -> 71.8 us (0.39)
  other arithmetic: 45.8 us -> 4.83 us
  matrix products: 53.4 us -> 20.7 us
  local copies, waits for them, and re-layouts: 32.2 us -> 7.59 us
  waiting for transfers between devices: 38.5 us -> 15.5 us
  between operations: 14.8 us -> 0.93 us
  Pallas kernels: 0 us -> 13.1 us
  starting transfers between devices: 0.23 us -> 8.67 us
    another operation x9 -> x1, other arithmetic: 40.8 us -> 0.11 us  [body(): jnp.stack([large(solved_two, below_left, (0, 0)).reshape(rows, share, -1)...]
    psum x1 -> x0, waiting for transfers between devices: 22.5 us -> none  [body(): lax.psum((matmul(solved_two.T, panel_two_all), matmul(solved_two.T, panel...]
    dot_general x16, matrix products: 39 us -> 20.7 us  [large(): lax.dot_general(left, right, ((contract[:1], contract[1:]), ((), ())), pr...]
    ppermute x0 -> x8, waiting for transfers between devices: none -> 15.5 us  [swap(): return lax.ppermute(values, axis, [(at, at ^ bit) for at in range(size)])]
    another operation x21 -> x0, matrix products: 14.5 us -> none  [the longest x15 11.7 us: right_solve(): lax.linalg.triangular_solve(factor, values, left_side=False, lower=True)]
    all_gather x4 -> x0, waiting for transfers between devices: 13.4 us -> none  [the longest x1 11 us: body(): lax.all_gather(panel_two, 'col', axis=1, tiled=True)]
    pallas_call x0 -> x2, Pallas kernels: none -> 13.1 us  [local_call(): pl.pallas_call(kernel, out_shape=[jax.ShapeDtypeStruct((size, size), jnp....]
    gather x4 -> x0, local copies, waits for them, and re-layouts: 9.74 us -> none  [halved(): return jnp.tril(square) - 0.5 * jnp.diag(jnp.diag(square))]
  transfers between devices with their start and end apart: 6 -> 8, of which waited for: 3 -> 5; matrix products, arithmetic and copies ran while one was open for 65% -> 28% of each run, Pallas kernels for 0% -> 8%
where the time goes in v1:
time: 71.8 us; the launch traced here: 71.2 us
  matrix products  20.7 us (29%)
  waiting for transfers between devices  15.5 us (22%)
  Pallas kernels  13.1 us (18%)
  starting transfers between devices  8.67 us (12%)
  local copies, waits for them, and re-layouts  7.59 us (11%)
  other arithmetic  4.83 us (7%)
  between operations  0.93 us (1%)
    dot_general x16, matrix products, large(): lax.dot_general(left, right, ((contract[:1], contract[1:]), ((), ())), pr...  20.7 us
    ppermute x8, waiting for transfers between devices, swap(): return lax.ppermute(values, axis, [(at, at ^ bit) for at in range(size)])  15.5 us
    pallas_call x2, Pallas kernels, local_call(): pl.pallas_call(kernel, out_shape=[jax.ShapeDtypeStruct((size, size), jnp....  13.1 us
    ppermute x8, starting transfers between devices, swap(): return lax.ppermute(values, axis, [(at, at ^ bit) for at in range(size)])  8.67 us
    unnamed x36, local copies, waits for them, and re-layouts  5.14 us
    add x3, other arithmetic, halve(): return keep + swap(give, axis, bit)  1.88 us
  transfers between devices with their start and end apart: 8, of which 5 were waited for; matrix products, arithmetic and copies ran while one was open for 28% of the time, Pallas kernels for 8%

profile of v1, /device:TPU:0, one launch (start us, length us, event | category | flops | bytes accessed | tf_op | source)
XLA Modules:
  0.0 71.2 jit_solution(15260081090054201837)
XLA Ops:
  0.6 3.1 %collective-permute-start = (f32[1024,128]{1,0:T(8,128)}, f32[1024,128]{1,0:T(8,128)}, u32[]{:S(2)}, u32[]{:S(2)}) collective-permute-start(f32[1024,128]{1,0:T(8,128)} %param.30), channel_id=1, source_target_pairs={{0,4},{4,0},{1,5},{5,1},{2,6},{6,2},{3,7},{7,3},{8,12},{12,8},{9,1... | collective-permute-start | bytes 1572872 | tf_op jit(solution)/shard_map/ppermute | solution.py:134
  3.8 5.6 %shard_map.215 = (f32[256,256]{1,0:T(8,128)}, f32[256,256]{1,0:T(8,128)}, f32[256,256]{1,0:T(8,128)}) custom-call(f32[256,256]{1,0:T(8,128)} %two_ref.3, f32[256,256]{1,0:T(8,128)} %one_ref.3, f32[256,256]{1,0:T(8,128)} %cross_ref.3), custom_call_target="tpu_custom_call" | custom-call | flops 2013265920 | bytes 1572864 | tf_op jit(solution)/shard_map/pallas_call | solution.py:123
  9.4 1.6 %fusion.18 = f32[256,1024]{1,0:T(8,128)S(1)} fusion(f32[1024,128]{1,0:T(8,128)S(1)} %copy-done.9, f32[256,256]{1,0:T(8,128)} %get-tuple-element.16.inv_two_ref, s32[]{:T(128)S(6)} %select_n.78), kind=kOutput, calls=%fused_computation.36 | convolution fusion | flops 201326592 | bytes 1703940 | tf_op jit(solution)/shard_map/dot_general | solution.py:10
  11.1 1.6 %fusion.15 = f32[256,1024]{1,0:T(8,128)S(1)} fusion(f32[1024,128]{1,0:T(8,128)S(1)} %copy-done.10, f32[256,256]{1,0:T(8,128)} %get-tuple-element.17.inv_one_ref, s32[]{:T(128)S(6)} %select_n.78), kind=kOutput, calls=%fused_computation.33 | convolution fusion | flops 201326592 | bytes 1703940 | tf_op jit(solution)/shard_map/dot_general | solution.py:10
  12.7 4.1 %collective-permute-done = f32[1024,128]{1,0:T(8,128)} collective-permute-done((f32[1024,128]{1,0:T(8,128)}, f32[1024,128]{1,0:T(8,128)}, u32[]{:S(2)}, u32[]{:S(2)}) %collective-permute-start) | collective-permute-done | bytes 524320 | tf_op jit(solution)/shard_map/ppermute | solution.py:134
  16.8 1.7 %convolution_add_fusion.1 = f32[256,1024]{1,0:T(8,128)S(1)} fusion(f32[256,1024]{1,0:T(8,128)S(1)} %fusion.18, f32[1024,128]{1,0:T(8,128)} %collective-permute-done, f32[256,256]{1,0:T(8,128)S(1)} %copy-done.12, s32[]{:T(128)S(6)} %select_n.79), kind=kOutput, calls=%fused_computation.4 | convolution fusion | flops 201588736 | bytes 2752516 | tf_op jit(solution)/shard_map/dot_general | solution.py:10
  19.1 1.1 %fusion.38 = f32[256,512]{1,0:T(8,128)S(1)} fusion(f32[256,1024]{1,0:T(8,128)S(1)} %convolution_add_fusion.1, f32[1024,512]{1,0:T(8,128)S(1)} %copy-done), kind=kOutput, calls=%fused_computation.58 | convolution fusion | flops 805306368 | bytes 3670016 | tf_op jit(solution)/shard_map/dot_general | solution.py:10
  20.2 7.0 %collective-permute-done.1 = f32[1024,128]{1,0:T(8,128)} collective-permute-done((f32[1024,128]{1,0:T(8,128)}, f32[1024,128]{1,0:T(8,128)}, u32[]{:S(2)}, u32[]{:S(2)}) %collective-permute-start.1) | collective-permute-done | bytes 524320 | tf_op jit(solution)/shard_map/ppermute | solution.py:134
  27.2 1.7 %fusion.1 = f32[1024,256]{0,1:T(8,128)S(1)} fusion(f32[1024,256]{0,1:T(8,128)S(1)} %fusion.37, f32[256,1024]{1,0:T(8,128)S(1)} %fusion.15, f32[1024,128]{1,0:T(8,128)} %collective-permute-done.1, f32[256,256]{1,0:T(8,128)S(1)} %copy-done.13, s32[]{:T(128)S(6)} %select_n.79), kind=kOutput, calls=%fused_computation.3 | convolution fusion | flops 201850880 | bytes 3801092 | tf_op jit(solution)/shard_map/dot_general | solution.py:10
  28.9 1.1 %fusion.39 = f32[256,512]{1,0:T(8,128)S(1)} fusion(f32[1024,256]{0,1:T(8,128)S(1)} %fusion.1, f32[1024,512]{1,0:T(8,128)S(1)} %copy-done), kind=kOutput, calls=%fused_computation.59 | convolution fusion | flops 805306368 | bytes 3670016 | tf_op jit(solution)/shard_map/dot_general | solution.py:10
  33.9 1.8 %collective-permute-start.5 = (f32[384,128]{1,0:T(8,128)S(1)}, f32[384,128]{1,0:T(8,128)S(1)}, u32[]{:S(2)}, u32[]{:S(2)}) collective-permute-start(f32[384,128]{1,0:T(8,128)S(1)} %bitcast_add_fusion.1), channel_id=1, source_target_pairs={{0,16},{8,24},{16,0},{24,8},{1,17},{9,25},{17,1},{25,9},{2,18},{10... | collective-permute-start | bytes 589832 | tf_op jit(solution)/shard_map/ppermute | solution.py:134
  35.7 2.6 %subtract_subtract_fusion = f32[1024,512]{1,0:T(8,128)} fusion(f32[1024,512]{1,0:T(8,128)S(1)} %copy-done.7, f32[1024,512]{1,0:T(8,128)S(1)} %fusion.36, f32[1024,256]{0,1:T(8,128)S(1)} %fusion.1, f32[256,512]{1,0:T(8,128)S(1)} %copy-done.3), kind=kOutput, calls=%fused_computation | convolution fusion | flops 806354944 | bytes 7864320 | tf_op jit(solution)/shard_map/dot_general | solution.py:10
  38.2 2.8 %collective-permute-done.5 = f32[384,128]{1,0:T(8,128)S(1)} collective-permute-done((f32[384,128]{1,0:T(8,128)S(1)}, f32[384,128]{1,0:T(8,128)S(1)}, u32[]{:S(2)}, u32[]{:S(2)}) %collective-permute-start.5) | collective-permute-done | bytes 196640 | tf_op jit(solution)/shard_map/ppermute | solution.py:134
  41.1 1.8 %collective-permute-start.6 = (f32[384,128]{1,0:T(8,128)S(1)}, f32[384,128]{1,0:T(8,128)S(1)}, u32[]{:S(2)}, u32[]{:S(2)}) collective-permute-start(f32[384,128]{1,0:T(8,128)S(1)} %add.82), channel_id=1, source_target_pairs={{0,4},{4,0},{1,5},{5,1},{2,6},{6,2},{3,7},{7,3},{8,12},{12,8},{9,1... | collective-permute-start | bytes 589832 | tf_op jit(solution)/shard_map/ppermute | solution.py:134
  44.5 1.5 %collective-permute-start.3 = (f32[1,2,64,512]{3,2,1,0:T(8,128)}, f32[1,2,64,512]{3,2,1,0:T(8,128)}, u32[]{:S(2)}, u32[]{:S(2)}) collective-permute-start(f32[1,2,64,512]{3,2,1,0:T(8,128)} %constant_dynamic-slice_fusion.1), channel_id=1, source_target_pairs={{0,16},{8,24},{16,0},{24,8},{1,17},{9,25},{17,1},{25,9},{2,18},{10... | collective-permute-start | bytes 786440 | tf_op jit(solution)/shard_map/ppermute | solution.py:134
  46.0 1.4 %collective-permute-done.6 = f32[384,128]{1,0:T(8,128)S(1)} collective-permute-done((f32[384,128]{1,0:T(8,128)S(1)}, f32[384,128]{1,0:T(8,128)S(1)}, u32[]{:S(2)}, u32[]{:S(2)}) %collective-permute-start.6) | collective-permute-done | bytes 196640 | tf_op jit(solution)/shard_map/ppermute | solution.py:134
  49.1 2.0 %copy.28 = f32[1024,128]{1,0:T(8,128)} copy(f32[1024,128]{0,1:T(8,128)} %constant_dynamic-slice_fusion) | data formatting | bytes 1048576
  51.9 2.0 %copy.27 = f32[1024,128]{1,0:T(8,128)} copy(f32[1024,128]{0,1:T(8,128)} %dynamic-slice_bitcast_fusion) | data formatting | bytes 1048576
  54.0 1.8 %dynamic-slice_add_fusion = f32[1,2,64,512]{3,2,1,0:T(8,128)} fusion(f32[1,2,64,512]{3,2,1,0:T(8,128)} %collective-permute-done.3, f32[2,2,64,512]{3,2,1,0:T(8,128)} %copy-done.5, s32[]{:T(128)S(6)} %select_n.85), kind=kLoop, calls=%fused_computation.17 | loop fusion | flops 65536 | bytes 786436 | tf_op jit(solution)/shard_map/add | solution.py:169
  57.8 7.4 %shard_map.216 = (f32[256,256]{1,0:T(8,128)}, f32[256,256]{1,0:T(8,128)}, f32[256,256]{1,0:T(8,128)}, f32[256,256]{1,0:T(8,128)}, f32[256,256]{1,0:T(8,128)}) custom-call(f32[256,256]{1,0:T(8,128)} %two_ref.3, f32[256,256]{1,0:T(8,128)} %one_ref.3, f32[256,256]{1,0:T(8,128)} %cross_ref.3, f32[256,256]{1,0:T(8,128)} %get-tuple-element.16.inv_two_ref, ...), custom_call_target="tpu_custom_call" | custom-call | flops 2013265920 | bytes 3670016 | tf_op jit(solution)/shard_map/pallas_call | solution.py:123
  65.2 1.1 %fusion.20 = f32[64,512]{1,0:T(8,128)S(1)} fusion(f32[256,512]{1,0:T(8,128)S(1)} %copy-done.4, f32[256,256]{1,0:T(8,128)} %get-tuple-element.21, s32[]{:T(128)S(6)} %select_n.93), kind=kOutput, calls=%fused_computation.40 | convolution fusion | flops 50331648 | bytes 720900 | tf_op jit(solution)/shard_map/dot_general | solution.py:10
  66.4 1.1 %fusion.26 = f32[64,512]{1,0:T(8,128)S(1)} fusion(f32[256,512]{1,0:T(8,128)S(1)} %copy-done.2, f32[256,256]{1,0:T(8,128)} %get-tuple-element.19, s32[]{:T(128)S(6)} %select_n.93), kind=kOutput, calls=%fused_computation.44 | convolution fusion | flops 50331648 | bytes 720900 | tf_op jit(solution)/shard_map/dot_general | solution.py:10
  67.5 1.9 %fusion.6 = f32[64,512]{1,0:T(8,128)} fusion(f32[64,512]{1,0:T(8,128)S(1)} %fusion.20, f32[64,512]{1,0:T(8,128)S(1)} %copy-done.15, f32[1,2,64,512]{3,2,1,0:T(8,128)S(1)} %copy-done.8, f32[256,512]{1,0:T(8,128)S(1)} %copy-done.2, f32[256,256]{1,0:T(8,128)} %get-tuple-element.29, s32[]{:T(128)S(6)} %select_n.93), kind=kOutput, calls=%fused_computation.25 | convolution fusion | flops 50429952 | bytes 1179652 | tf_op jit(solution)/shard_map/dot_general | solution.py:10
  69.4 1.8 %fusion.9 = f32[64,512]{1,0:T(8,128)} fusion(f32[64,512]{1,0:T(8,128)S(1)} %fusion.26, f32[64,512]{1,0:T(8,128)S(1)} %copy-done.16, f32[1,2,64,512]{3,2,1,0:T(8,128)S(1)} %copy-done.8, f32[256,512]{1,0:T(8,128)S(1)} %copy-done.4, f32[256,256]{1,0:T(8,128)} %get-tuple-element.29, s32[]{:T(128)S(6)} %select_n.93), kind=kOutput, calls=%fused_computation.29 | convolution fusion | flops 50429952 | bytes 1114116 | tf_op jit(solution)/shard_map/dot_general | solution.py:10
  (61 shorter events, 10.6 us)
Async XLA Ops:
  0.6 18.5 %copy-start = (f32[1024,512]{1,0:T(8,128)S(1)}, f32[1024,512]{1,0:T(8,128)}, u32[]{:S(2)}) copy-start(f32[1024,512]{1,0:T(8,128)} %param.21) | copy-start | bytes 6291460
  0.6 16.2 %collective-permute-start = (f32[1024,128]{1,0:T(8,128)}, f32[1024,128]{1,0:T(8,128)}, u32[]{:S(2)}, u32[]{:S(2)}) collective-permute-start(f32[1024,128]{1,0:T(8,128)} %param.30), channel_id=1, source_target_pairs={{0,4},{4,0},{1,5},{5,1},{2,6},{6,2},{3,7},{7,3},{8,12},{12,8},{9,1... | collective-permute-start | bytes 1572872 | tf_op jit(solution)/shard_map/ppermute | solution.py:134
  3.7 23.5 %collective-permute-start.1 = (f32[1024,128]{1,0:T(8,128)}, f32[1024,128]{1,0:T(8,128)}, u32[]{:S(2)}, u32[]{:S(2)}) collective-permute-start(f32[1024,128]{1,0:T(8,128)} %param.31), channel_id=1, source_target_pairs={{0,4},{4,0},{1,5},{5,1},{2,6},{6,2},{3,7},{7,3},{8,12},{12,8},{9,1... | collective-permute-start | bytes 1572872 | tf_op jit(solution)/shard_map/ppermute | solution.py:134
  3.8 5.7 %copy-start.9 = (f32[1024,128]{1,0:T(8,128)S(1)}, f32[1024,128]{1,0:T(8,128)}, u32[]{:S(2)}) copy-start(f32[1024,128]{1,0:T(8,128)} %param.30) | copy-start | bytes 1572868
  3.8 7.3 %copy-start.10 = (f32[1024,128]{1,0:T(8,128)S(1)}, f32[1024,128]{1,0:T(8,128)}, u32[]{:S(2)}) copy-start(f32[1024,128]{1,0:T(8,128)} %param.31) | copy-start | bytes 1572868
  9.4 7.4 %copy-start.12 = (f32[256,256]{1,0:T(8,128)S(1)}, f32[256,256]{1,0:T(8,128)}, u32[]{:S(2)}) copy-start(f32[256,256]{1,0:T(8,128)} %get-tuple-element.16.inv_two_ref) | copy-start | bytes 786436
  11.1 7.4 %copy-start.14 = (f32[256,256]{1,0:T(8,128)S(1)}, f32[256,256]{1,0:T(8,128)}, u32[]{:S(2)}) copy-start(f32[256,256]{1,0:T(8,128)} %get-tuple-element.18) | copy-start | bytes 786436
  19.1 8.1 %copy-start.13 = (f32[256,256]{1,0:T(8,128)S(1)}, f32[256,256]{1,0:T(8,128)}, u32[]{:S(2)}) copy-start(f32[256,256]{1,0:T(8,128)} %get-tuple-element.17.inv_one_ref) | copy-start | bytes 786436
  28.9 1.1 %copy-start.6 = (f32[1024,128]{1,0:T(8,128)S(1)}, f32[1024,128]{1,0:T(8,128)}, u32[]{:S(2)}) copy-start(f32[1024,128]{1,0:T(8,128)} %param.23) | copy-start | bytes 1572868
  30.6 1.0 %copy-start.11 = (f32[1024,128]{1,0:T(8,128)S(1)}, f32[1024,128]{1,0:T(8,128)}, u32[]{:S(2)}) copy-start(f32[1024,128]{1,0:T(8,128)} %param.22) | copy-start | bytes 1572868
  31.4 1.4 %copy-start.1 = (f32[256,512]{1,0:T(8,128)S(1)}, f32[256,512]{1,0:T(8,128)}, u32[]{:S(2)}) copy-start(f32[256,512]{1,0:T(8,128)} %param.19) | copy-start | bytes 1572868
  31.4 11.5 %collective-permute-start.2 = (f32[2,2,64,512]{3,2,1,0:T(8,128)S(1)}, f32[2,2,64,512]{3,2,1,0:T(8,128)S(1)}, u32[]{:S(2)}, u32[]{:S(2)}) collective-permute-start(f32[2,2,64,512]{3,2,1,0:T(8,128)S(1)} %bitcast.62), channel_id=1, source_target_pairs={{0,8},{8,0},{16,24},{24,16},{1,9},{9,1},{17,25},{25,17},{2,10},{10... | collective-permute-start | bytes 1572872 | tf_op jit(solution)/shard_map/ppermute | solution.py:134
  32.3 3.3 %copy-start.3 = (f32[256,512]{1,0:T(8,128)S(1)}, f32[256,512]{1,0:T(8,128)}, u32[]{:S(2)}) copy-start(f32[256,512]{1,0:T(8,128)} %param.20) | copy-start | bytes 1572868
  32.4 3.3 %copy-start.7 = (f32[1024,512]{1,0:T(8,128)S(1)}, f32[1024,512]{1,0:T(8,128)}, u32[]{:S(2)}) copy-start(f32[1024,512]{1,0:T(8,128)} %param.29) | copy-start | bytes 6291460
  32.4 1.5 %collective-permute-start.4 = (f32[384,128]{1,0:T(8,128)S(1)}, f32[384,128]{1,0:T(8,128)S(1)}, u32[]{:S(2)}, u32[]{:S(2)}) collective-permute-start(f32[384,128]{1,0:T(8,128)S(1)} %dynamic-slice_bitcast_fusion.1), channel_id=1, source_target_pairs={{0,8},{8,0},{16,24},{24,16},{1,9},{9,1},{17,25},{25,17},{2,10},{10... | collective-permute-start | bytes 589832 | tf_op jit(solution)/shard_map/ppermute | solution.py:134
  33.9 7.2 %collective-permute-start.5 = (f32[384,128]{1,0:T(8,128)S(1)}, f32[384,128]{1,0:T(8,128)S(1)}, u32[]{:S(2)}, u32[]{:S(2)}) collective-permute-start(f32[384,128]{1,0:T(8,128)S(1)} %bitcast_add_fusion.1), channel_id=1, source_target_pairs={{0,16},{8,24},{16,0},{24,8},{1,17},{9,25},{17,1},{25,9},{2,18},{10... | collective-permute-start | bytes 589832 | tf_op jit(solution)/shard_map/ppermute | solution.py:134
  41.1 6.3 %collective-permute-start.6 = (f32[384,128]{1,0:T(8,128)S(1)}, f32[384,128]{1,0:T(8,128)S(1)}, u32[]{:S(2)}, u32[]{:S(2)}) collective-permute-start(f32[384,128]{1,0:T(8,128)S(1)} %add.82), channel_id=1, source_target_pairs={{0,4},{4,0},{1,5},{5,1},{2,6},{6,2},{3,7},{7,3},{8,12},{12,8},{9,1... | collective-permute-start | bytes 589832 | tf_op jit(solution)/shard_map/ppermute | solution.py:134
  44.5 9.5 %collective-permute-start.3 = (f32[1,2,64,512]{3,2,1,0:T(8,128)}, f32[1,2,64,512]{3,2,1,0:T(8,128)}, u32[]{:S(2)}, u32[]{:S(2)}) collective-permute-start(f32[1,2,64,512]{3,2,1,0:T(8,128)} %constant_dynamic-slice_fusion.1), channel_id=1, source_target_pairs={{0,16},{8,24},{16,0},{24,8},{1,17},{9,25},{17,1},{25,9},{2,18},{10... | collective-permute-start | bytes 786440 | tf_op jit(solution)/shard_map/ppermute | solution.py:134
  48.2 7.5 %collective-permute-start.7 = (f32[384,256]{1,0:T(8,128)}, f32[384,256]{1,0:T(8,128)}, u32[]{:S(2)}, u32[]{:S(2)}) collective-permute-start(f32[384,256]{1,0:T(8,128)} %pad_maximum_fusion.2), channel_id=1, source_target_pairs={{0,8},{8,0},{16,24},{24,16},{1,9},{9,1},{17,25},{25,17},{2,10},{10... | collective-permute-start | bytes 1179656 | tf_op jit(solution)/shard_map/ppermute | solution.py:134
  57.8 7.4 %copy-start.4 = (f32[256,512]{1,0:T(8,128)S(1)}, f32[256,512]{1,0:T(8,128)}, u32[]{:S(2)}) copy-start(f32[256,512]{1,0:T(8,128)} %param.20) | copy-start | bytes 1572868
  57.8 8.6 %copy-start.2 = (f32[256,512]{1,0:T(8,128)S(1)}, f32[256,512]{1,0:T(8,128)}, u32[]{:S(2)}) copy-start(f32[256,512]{1,0:T(8,128)} %param.19) | copy-start | bytes 1572868
  57.8 9.7 %copy-start.8 = (f32[1,2,64,512]{3,2,1,0:T(8,128)S(1)}, f32[1,2,64,512]{3,2,1,0:T(8,128)}, u32[]{:S(2)}) copy-start(f32[1,2,64,512]{3,2,1,0:T(8,128)} %dynamic-slice_add_fusion) | copy-start | bytes 786436
  57.8 9.7 %copy-start.15 = (f32[64,512]{1,0:T(8,128)S(1)}, f32[64,512]{1,0:T(8,128)}, u32[]{:S(2)}) copy-start(f32[64,512]{1,0:T(8,128)} %param.28) | copy-start | bytes 393220
  65.2 4.2 %copy-start.16 = (f32[64,512]{1,0:T(8,128)S(1)}, f32[64,512]{1,0:T(8,128)}, u32[]{:S(2)}) copy-start(f32[64,512]{1,0:T(8,128)} %param.27) | copy-start | bytes 393220
  (1 other events, 0.8 us)

commit v2 on v1

--- a/solution.py
+++ b/solution.py
@@ -81,7 +81,45 @@
     grad_two_ref,
     grad_one_ref,
     grad_cross_ref,
-    grams_ref,
+    place_ref,
+    *rest,
+):
+    grams, outs = rest[:-5], rest[-5:]
+    chain(
+        two_ref,
+        one_ref,
+        cross_ref,
+        inv_two_ref,
+        inv_one_ref,
+        grad_two_ref,
+        grad_one_ref,
+        grad_cross_ref,
+        joined(grams, place_ref),
+        *outs,
+    )
+
+
+def joined(grams, place_ref):
+    if len(grams) == 1:
+        return grams[0][...]
+    mine, beside, twin, across = [gram[...] for gram in grams]
+    left = place_ref[0] == 0
+    upper = place_ref[1] == 0
+    own = jnp.concatenate([jnp.where(left, mine, beside), jnp.where(left, beside, mine)], axis=1)
+    far = jnp.concatenate([jnp.where(left, twin, across), jnp.where(left, across, twin)], axis=1)
+    return jnp.concatenate([jnp.where(upper, own, far), jnp.where(upper, far, own)], axis=0)
+
+
+def chain(
+    two_ref,
+    one_ref,
+    cross_ref,
+    inv_two_ref,
+    inv_one_ref,
+    grad_two_ref,
+    grad_one_ref,
+    grad_cross_ref,
+    grams,
     sym_two_ref,
     sym_one_ref,
     half_two_ref,
@@ -98,9 +136,9 @@
         spread = small(small(inverse, inner, (0, 0)), inverse)
         return spread + spread.T
 
-    gram_two = grams_ref[:size, :]
-    gram_cross = grams_ref[size : 2 * size, :]
-    gram_below = grams_ref[2 * size :, :]
+    gram_two = grams[:size, :]
+    gram_cross = grams[size : 2 * size, :]
+    gram_below = grams[2 * size :, :]
     sym_two = sym(
         two_ref[...], inv_two_ref[...], grad_two_ref[...] - jnp.where(lower, gram_two, 0.0)
     )
@@ -123,7 +161,10 @@
     return pl.pallas_call(
         kernel,
         out_shape=[jax.ShapeDtypeStruct((size, size), jnp.float32)] * count,
-        in_specs=[pl.BlockSpec(memory_space=pltpu.VMEM)] * len(operands),
+        in_specs=[
+            pl.BlockSpec(memory_space=pltpu.SMEM if operand.ndim == 1 else pltpu.VMEM)
+            for operand in operands
+        ],
         out_specs=[pl.BlockSpec(memory_space=pltpu.VMEM)] * count,
         cost_estimate=pl.CostEstimate(flops=flops, bytes_accessed=moved, transcendentals=0),
     )(*operands)
@@ -142,13 +183,62 @@
     return [(values, at * width), (swap(values, axis, 1), (1 - at) * width)]
 
 
-def times(pieces, factor):
+def parted(values):
+    high = values.astype(jnp.bfloat16)
+    return high, (values - high.astype(jnp.float32)).astype(jnp.bfloat16)
+
+
+def product(left, right):
+    (left_high, left_low), (right_high, right_low) = parted(left), parted(right)
+
+    def single(one, other):
+        return jnp.dot(one, other, preferred_element_type=jnp.float32)
+
+    return (single(left_low, right_high) + single(left_high, right_low)) + single(
+        left_high, right_high
+    )
+
+
+def solve_kernel(count, starts_ref, inverse_ref, *refs):
+    pieces, extra, outs = refs[:count], refs[count:-count], refs[-count:]
     total = None
-    for values, start in pieces:
-        rows = lax.dynamic_slice_in_dim(factor, start, values.shape[1], 0)
-        part = large(values, rows, (1, 0))
+    for at, piece in enumerate(pieces):
+        width = piece.shape[1]
+        rows = inverse_ref[pl.ds(pl.multiple_of(starts_ref[at], width), width), :]
+        part = product(piece[...], rows)
         total = part if total is None else total + part
-    return total
+    if extra:
+        total = total - product(extra[0][...], extra[1][...])
+    outs[0][...] = total
+    if count > 1:
+        width = outs[1].shape[1]
+        outs[1][...] = jnp.where(starts_ref[0] == 0, total[:, :width], total[:, width:])
+
+
+def solve(pieces, inverse, *extra):
+    count = len(pieces)
+    rows, width = pieces[0][0].shape
+    size = inverse.shape[0]
+    block = rows // 4
+    starts = jnp.stack([jnp.asarray(start, jnp.int32) for _, start in pieces])
+
+    def tall(columns):
+        return pl.BlockSpec((block, columns), lambda step: (step, 0))
+
+    whole = pl.BlockSpec((size, size), lambda step: (0, 0))
+    widths = [size, width][:count]
+    return pl.pallas_call(
+        lambda *refs: solve_kernel(count, *refs),
+        grid=(4,),
+        out_shape=[jax.ShapeDtypeStruct((rows, columns), jnp.float32) for columns in widths],
+        in_specs=[pl.BlockSpec(memory_space=pltpu.SMEM), whole]
+        + [tall(values.shape[1]) for values, _ in pieces]
+        + ([tall(size), whole] if extra else []),
+        out_specs=[tall(columns) for columns in widths],
+        cost_estimate=pl.CostEstimate(
+            flops=6 * rows * size * size, bytes_accessed=12 * rows * size, transcendentals=0
+        ),
+    )(starts, inverse, *[values for values, _ in pieces], *extra)
 
 
 def assembled(values, axis):
@@ -184,16 +274,19 @@
 def row_sum(values, axis, columns):
     size = lax.axis_size(axis)
     if size & (size - 1) or size < 2:
-        return assembled(lax.psum(values, axis), columns)
+        return [assembled(lax.psum(values, axis), columns)]
     part = halve(values.reshape((2, -1) + values.shape[1:]), axis, 1)
     bit = 2
     while bit < size:
         part = part + swap(part, axis, bit)
         bit *= 2
+    if lax.axis_size(columns) == 2:
+        beside = swap(part, columns, 1)
+        return [part, beside, swap(part, axis, 1), swap(beside, axis, 1)]
     part = assembled(part, columns)
     other = swap(part, axis, 1)
     even = lax.axis_index(axis) % 2 == 0
-    return jnp.concatenate([jnp.where(even, part, other), jnp.where(even, other, part)], axis=0)
+    return [jnp.concatenate([jnp.where(even, part, other), jnp.where(even, other, part)], axis=0)]
 
 
 def body(
@@ -226,8 +319,9 @@
     inv_two, inv_one, cross_inv = local_call(
         invert_kernel, (diag_two, diag_one, cross_tile), 3, 60 * cube
     )
-    solved_two = times(pieces_two, inv_two)
-    solved_one = times(pieces_one, inv_one) - large(solved_two, cross_inv, (1, 0))
+    solved_two, *own_two = solve(pieces_two, inv_two)
+    solved_one, *own_one = solve(pieces_one, inv_one, solved_two, cross_inv)
+    place = jnp.stack([lax.axis_index("col"), lax.axis_index("row") % 2]).astype(jnp.int32)
     partial = jnp.concatenate(
         [
             large(solved_two, panel_two, (0, 0)),
@@ -260,7 +354,8 @@
             grad_diag_two,
             grad_diag_one,
             grad_cross,
-            grams,
+            place,
+            *grams,
         ),
         5,
         60 * cube,
@@ -288,8 +383,8 @@
         half_two,
         half_one,
         out_cross,
-        lax.dynamic_slice_in_dim(solved_two, col_start, width, 1),
-        lax.dynamic_slice_in_dim(solved_one, col_start, width, 1),
+        own_two[0] if own_two else lax.dynamic_slice_in_dim(solved_two, col_start, width, 1),
+        own_one[0] if own_one else lax.dynamic_slice_in_dim(solved_one, col_start, width, 1),
     )
 
 

time: 71.8 us -> 69.8 us (0.972)
  Pallas kernels: 13.1 us -> 22 us
  local copies, waits for them, and re-layouts: 7.59 us -> 2.66 us
  matrix products: 20.7 us -> 16.3 us
  other arithmetic: 4.83 us -> 2.49 us
    pallas_call x0 -> x2, Pallas kernels: none -> 9.12 us  [solve(): pl.pallas_call(lambda *refs: solve_kernel(count, *refs), grid=(4,), out_s...]
    dot_general x16 -> x11, matrix products: 20.7 us -> 16.3 us  [large(): lax.dot_general(left, right, ((contract[:1], contract[1:]), ((), ())), pr...]
    unnamed x36 -> x32, local copies, waits for them, and re-layouts: 5.14 us -> 2.59 us
    concatenate x2 -> x0, other arithmetic: 1.71 us -> none  [the longest x1 0.94 us: row_sum(): jnp.concatenate([jnp.where(even, part, other), jnp.where(even, other, par...]
    dynamic_slice x2 -> x0, local copies, waits for them, and re-layouts: 1.68 us -> none  [the longest x1 0.85 us: body(): lax.dynamic_slice_in_dim(solved_two, col_start, width, 1)]
    another operation x0 -> x2, other arithmetic: none -> 1.17 us  [the longest x1 0.58 us: solve(): starts = jnp.stack([jnp.asarray(start, jnp.int32) for _, start in pieces])]
    select_n x2 -> x0, other arithmetic: 1.08 us -> none  [the longest x1 1.05 us: row_sum(): jnp.where(even, part, other)]
    ppermute x8 -> x9, starting transfers between devices: 8.67 us -> 9.13 us  [swap(): return lax.ppermute(values, axis, [(at, at ^ bit) for at in range(size)])]
  transfers between devices with their start and end apart: 8 -> 9, of which waited for: 5 -> 4; matrix products, arithmetic and copies ran while one was open for 28% -> 15% of each run, Pallas kernels for 8% -> 25%
where the time goes in v2:
time: 69.8 us; the launch traced here: 69.3 us
  Pallas kernels  22 us (32%)
  matrix products  16.3 us (23%)
  waiting for transfers between devices  15.8 us (23%)
  starting transfers between devices  9.13 us (13%)
  local copies, waits for them, and re-layouts  2.66 us (4%)
  other arithmetic  2.49 us (4%)
  between operations  0.88 us (1%)
    dot_general x11, matrix products, large(): lax.dot_general(left, right, ((contract[:1], contract[1:]), ((), ())), pr...  16.3 us
    ppermute x9, waiting for transfers between devices, swap(): return lax.ppermute(values, axis, [(at, at ^ bit) for at in range(size)])  15.8 us
    pallas_call x2, Pallas kernels, local_call(): pl.pallas_call(kernel, out_shape=[jax.ShapeDtypeStruct((size, size), jnp....  12.9 us
    ppermute x9, starting transfers between devices, swap(): return lax.ppermute(values, axis, [(at, at ^ bit) for at in range(size)])  9.13 us
    pallas_call x2, Pallas kernels, solve(): pl.pallas_call(lambda *refs: solve_kernel(count, *refs), grid=(4,), out_s...  9.12 us
    unnamed x32, local copies, waits for them, and re-layouts  2.59 us
  transfers between devices with their start and end apart: 9, of which 4 were waited for; matrix products, arithmetic and copies ran while one was open for 15% of the time, Pallas kernels for 25%

profile of v2, /device:TPU:0, one launch (start us, length us, event | category | flops | bytes accessed | tf_op | source)
XLA Modules:
  0.0 69.3 jit_solution(7672463275063512970)
XLA Ops:
  0.6 3.1 %collective-permute-start = (f32[1024,128]{1,0:T(8,128)}, f32[1024,128]{1,0:T(8,128)}, u32[]{:S(2)}, u32[]{:S(2)}) collective-permute-start(f32[1024,128]{1,0:T(8,128)} %refs_2_.2), channel_id=1, source_target_pairs={{0,4},{4,0},{1,5},{5,1},{2,6},{6,2},{3,7},{7,3},{8,12},{12,8},{9,1... | collective-permute-start | bytes 1572872 | tf_op jit(solution)/shard_map/ppermute | solution.py:175
  5.0 5.6 %shard_map.215 = (f32[256,256]{1,0:T(8,128)}, f32[256,256]{1,0:T(8,128)}, f32[256,256]{1,0:T(8,128)}) custom-call(f32[256,256]{1,0:T(8,128)} %two_ref.3, f32[256,256]{1,0:T(8,128)} %one_ref.3, f32[256,256]{1,0:T(8,128)} %cross_ref.3), custom_call_target="tpu_custom_call" | custom-call | flops 2013265920 | bytes 1572864 | tf_op jit(solution)/shard_map/pallas_call | solution.py:161
  10.6 6.2 %collective-permute-done.refs_3_ = f32[1024,128]{1,0:T(8,128)} collective-permute-done((f32[1024,128]{1,0:T(8,128)}, f32[1024,128]{1,0:T(8,128)}, u32[]{:S(2)}, u32[]{:S(2)}) %collective-permute-start) | collective-permute-done | bytes 524320 | tf_op jit(solution)/shard_map/ppermute | solution.py:175
  16.8 4.3 %shard_map.216 = (f32[1024,256]{1,0:T(8,128)}, f32[1024,128]{1,0:T(8,128)}) custom-call(s32[2]{0:T(128)} %pad_add_fusion.refs_0_, f32[256,256]{1,0:T(8,128)} %get-tuple-element.20.refs_1_.inv_two_ref, f32[1024,128]{1,0:T(8,128)} %refs_2_.2, f32[1024,128]{1,0:T(8,128)} %collective-permute-done.refs_3_), custom_call_target="tpu_custom_call" | custom-call | flops 402653184 | bytes 3145728 | tf_op jit(solution)/shard_map/pallas_call | solution.py:230
  21.1 2.2 %fusion.20 = f32[256,128]{1,0:T(8,128)S(1)} fusion(f32[1024,256]{1,0:T(8,128)} %get-tuple-element.21.refs_4_, f32[1024,128]{1,0:T(8,128)S(1)} %copy-done.6), kind=kOutput, calls=%fused_computation.38 | convolution fusion | flops 201326592 | bytes 1703936 | tf_op jit(solution)/shard_map/dot_general | solution.py:10
  23.3 3.7 %collective-permute-done.1.refs_3_ = f32[1024,128]{1,0:T(8,128)S(1)} collective-permute-done((f32[1024,128]{1,0:T(8,128)}, f32[1024,128]{1,0:T(8,128)S(1)}, u32[]{:S(2)}, u32[]{:S(2)}) %collective-permute-start.1) | collective-permute-done | bytes 524320 | tf_op jit(solution)/shard_map/ppermute | solution.py:175
  27.9 4.8 %shard_map.217 = (f32[1024,256]{1,0:T(8,128)}, f32[1024,128]{1,0:T(8,128)}) custom-call(s32[2]{0:T(128)} %pad_add_fusion.refs_0_, f32[256,256]{1,0:T(8,128)} %get-tuple-element.22.refs_1_.inv_one_ref, f32[1024,128]{1,0:T(8,128)} %refs_2_.3, f32[1024,128]{1,0:T(8,128)} %copy-done.9, f32[1024,256]{1,0:T(8,128)} %get-tuple-element.21.refs_4_, ...), custom_call_target="tpu_custom_call" | custom-call | flops 402653184 | bytes 3145728 | tf_op jit(solution)/shard_map/pallas_call | solution.py:230
  32.7 2.3 %fusion.21 = f32[256,128]{1,0:T(8,128)S(1)} fusion(f32[1024,256]{1,0:T(8,128)} %get-tuple-element.24, f32[1024,128]{1,0:T(8,128)S(1)} %copy-done.6), kind=kOutput, calls=%fused_computation.39 | convolution fusion | flops 201326592 | bytes 1703936 | tf_op jit(solution)/shard_map/dot_general | solution.py:10
  35.0 1.1 %fusion.18 = f32[256,512]{1,0:T(8,128)S(1)} fusion(f32[1024,256]{1,0:T(8,128)S(1)} %copy-done.2, f32[1024,512]{1,0:T(8,128)S(1)} %copy-done), kind=kOutput, calls=%fused_computation.36 | convolution fusion | flops 805306368 | bytes 3670016 | tf_op jit(solution)/shard_map/dot_general | solution.py:10
  36.4 1.0 %fusion.19 = f32[256,128]{1,0:T(8,128)S(1)} fusion(f32[1024,256]{1,0:T(8,128)S(1)} %copy-done.1, f32[1024,128]{1,0:T(8,128)S(1)} %copy-done.8), kind=kOutput, calls=%fused_computation.37 | convolution fusion | flops 201326592 | bytes 1703936 | tf_op jit(solution)/shard_map/dot_general | solution.py:10
  37.5 1.1 %fusion.17 = f32[256,512]{1,0:T(8,128)S(1)} fusion(f32[1024,256]{1,0:T(8,128)S(1)} %copy-done.1, f32[1024,512]{1,0:T(8,128)S(1)} %copy-done), kind=kOutput, calls=%fused_computation.35 | convolution fusion | flops 805306368 | bytes 3670016 | tf_op jit(solution)/shard_map/dot_general | solution.py:10
  39.4 1.8 %collective-permute-start.5 = (f32[384,128]{1,0:T(8,128)S(1)}, f32[384,128]{1,0:T(8,128)S(1)}, u32[]{:S(2)}, u32[]{:S(2)}) collective-permute-start(f32[384,128]{1,0:T(8,128)S(1)} %bitcast_add_fusion.1), channel_id=1, source_target_pairs={{0,16},{8,24},{16,0},{24,8},{1,17},{9,25},{17,1},{25,9},{2,18},{10... | collective-permute-start | bytes 589832 | tf_op jit(solution)/shard_map/ppermute | solution.py:175
  41.2 1.0 %fusion.16 = f32[1024,512]{1,0:T(8,128)S(1)} fusion(f32[1024,256]{1,0:T(8,128)S(1)} %copy-done.1, f32[256,512]{1,0:T(8,128)S(1)} %copy-done.3), kind=kOutput, calls=%fused_computation.34 | convolution fusion | flops 805306368 | bytes 3670016 | tf_op jit(solution)/shard_map/dot_general | solution.py:10
  42.2 4.1 %collective-permute-done.5 = f32[384,128]{1,0:T(8,128)S(1)} collective-permute-done((f32[384,128]{1,0:T(8,128)S(1)}, f32[384,128]{1,0:T(8,128)S(1)}, u32[]{:S(2)}, u32[]{:S(2)}) %collective-permute-start.5) | collective-permute-done | bytes 196640 | tf_op jit(solution)/shard_map/ppermute | solution.py:175
  46.3 1.8 %collective-permute-start.6 = (f32[384,128]{1,0:T(8,128)S(1)}, f32[384,128]{1,0:T(8,128)S(1)}, u32[]{:S(2)}, u32[]{:S(2)}) collective-permute-start(f32[384,128]{1,0:T(8,128)S(1)} %add.57.rest_0_), channel_id=1, source_target_pairs={{0,4},{4,0},{1,5},{5,1},{2,6},{6,2},{3,7},{7,3},{8,12},{12,8},{9,1... | collective-permute-start | bytes 589832 | tf_op jit(solution)/shard_map/ppermute | solution.py:175
  48.1 2.5 %subtract_subtract_fusion = f32[1024,512]{1,0:T(8,128)} fusion(f32[1024,512]{1,0:T(8,128)S(1)} %copy-done.7, f32[1024,512]{1,0:T(8,128)S(1)} %fusion.16, f32[1024,256]{1,0:T(8,128)S(1)} %copy-done.2, f32[256,512]{1,0:T(8,128)S(1)} %copy-done.4), kind=kOutput, calls=%fused_computation | convolution fusion | flops 806354944 | bytes 7864320 | tf_op jit(solution)/shard_map/dot_general | solution.py:10
  50.7 1.7 %collective-permute-done.6.rest_1_ = f32[384,128]{1,0:T(8,128)S(1)} collective-permute-done((f32[384,128]{1,0:T(8,128)S(1)}, f32[384,128]{1,0:T(8,128)S(1)}, u32[]{:S(2)}, u32[]{:S(2)}) %collective-permute-start.6) | collective-permute-done | bytes 196640 | tf_op jit(solution)/shard_map/ppermute | solution.py:175
  53.3 1.8 %collective-permute-start.3 = (f32[1,2,64,512]{3,2,1,0:T(8,128)S(1)}, f32[1,2,64,512]{3,2,1,0:T(8,128)}, u32[]{:S(2)}, u32[]{:S(2)}) collective-permute-start(f32[1,2,64,512]{3,2,1,0:T(8,128)S(1)} %constant_dynamic-slice_fusion), channel_id=1, source_target_pairs={{0,16},{8,24},{16,0},{24,8},{1,17},{9,25},{17,1},{25,9},{2,18},{10... | collective-permute-start | bytes 786440 | tf_op jit(solution)/shard_map/ppermute | solution.py:175
  55.8 7.3 %shard_map.218 = (f32[256,256]{1,0:T(8,128)}, f32[256,256]{1,0:T(8,128)}, f32[256,256]{1,0:T(8,128)}, f32[256,256]{1,0:T(8,128)}, f32[256,256]{1,0:T(8,128)}) custom-call(f32[256,256]{1,0:T(8,128)} %two_ref.3, f32[256,256]{1,0:T(8,128)} %one_ref.3, f32[256,256]{1,0:T(8,128)} %cross_ref.3, f32[256,256]{1,0:T(8,128)} %get-tuple-element.20.refs_1_.inv_two_ref, ...), custom_call_target="tpu_custom_call" | custom-call | flops 2013265920 | bytes 4718592 | tf_op jit(solution)/shard_map/pallas_call | solution.py:161
  63.1 1.2 %fusion.7 = f32[64,512]{1,0:T(8,128)S(1)} fusion(f32[256,512]{1,0:T(8,128)S(1)} %copy-done.4, f32[256,256]{1,0:T(8,128)} %get-tuple-element.27, s32[]{:T(128)S(6)} %select_n.51), kind=kOutput, calls=%fused_computation.22 | convolution fusion | flops 50331648 | bytes 720900 | tf_op jit(solution)/shard_map/dot_general | solution.py:10
  64.3 1.1 %fusion.9 = f32[64,512]{1,0:T(8,128)S(1)} fusion(f32[256,512]{1,0:T(8,128)S(1)} %copy-done.4, f32[256,256]{1,0:T(8,128)} %get-tuple-element.17, s32[]{:T(128)S(6)} %select_n.51), kind=kOutput, calls=%fused_computation.24 | convolution fusion | flops 50331648 | bytes 720900 | tf_op jit(solution)/shard_map/dot_general | solution.py:10
  65.4 1.1 %dynamic-slice_add_fusion = f32[1,2,64,512]{3,2,1,0:T(8,128)S(1)} fusion(f32[1,2,64,512]{3,2,1,0:T(8,128)} %collective-permute-done.3, f32[2,2,64,512]{3,2,1,0:T(8,128)} %copy-done.5, s32[]{:T(128)S(6)} %select_n.49), kind=kLoop, calls=%fused_computation.14 | loop fusion | flops 65536 | bytes 786436 | tf_op jit(solution)/shard_map/add | solution.py:259
  66.5 1.0 %fusion = f32[64,512]{1,0:T(8,128)} fusion(f32[64,512]{1,0:T(8,128)S(1)} %fusion.7, f32[256,512]{1,0:T(8,128)S(1)} %copy-done.3, f32[64,512]{1,0:T(8,128)S(1)} %copy-done.12, f32[1,2,64,512]{3,2,1,0:T(8,128)S(1)} %dynamic-slice_add_fusion, f32[256,256]{1,0:T(8,128)S(1)} %copy-done.11, s32[]{:T(128)S(6)} %select_n.51), kind=kOutput, calls=%fused_computation.6 | convolution fusion | flops 50429952 | bytes 1179652 | tf_op jit(solution)/shard_map/dot_general | solution.py:10
  67.5 1.8 %fusion.1 = f32[64,512]{1,0:T(8,128)} fusion(f32[64,512]{1,0:T(8,128)S(1)} %fusion.9, f32[256,512]{1,0:T(8,128)S(1)} %copy-done.3, f32[64,512]{1,0:T(8,128)S(1)} %copy-done.13, f32[1,2,64,512]{3,2,1,0:T(8,128)S(1)} %dynamic-slice_add_fusion, f32[256,256]{1,0:T(8,128)} %get-tuple-element.25, s32[]{:T(128)S(6)} %select_n.51), kind=kOutput, calls=%fused_computation.8 | convolution fusion | flops 50429952 | bytes 1114116 | tf_op jit(solution)/shard_map/dot_general | solution.py:10
  (52 shorter events, 4.8 us)
Async XLA Ops:
  0.6 34.4 %copy-start = (f32[1024,512]{1,0:T(8,128)S(1)}, f32[1024,512]{1,0:T(8,128)}, u32[]{:S(2)}) copy-start(f32[1024,512]{1,0:T(8,128)} %param.21) | copy-start | bytes 6291460
  0.6 16.2 %collective-permute-start = (f32[1024,128]{1,0:T(8,128)}, f32[1024,128]{1,0:T(8,128)}, u32[]{:S(2)}, u32[]{:S(2)}) collective-permute-start(f32[1024,128]{1,0:T(8,128)} %refs_2_.2), channel_id=1, source_target_pairs={{0,4},{4,0},{1,5},{5,1},{2,6},{6,2},{3,7},{7,3},{8,12},{12,8},{9,1... | collective-permute-start | bytes 1572872 | tf_op jit(solution)/shard_map/ppermute | solution.py:175
  3.7 23.4 %collective-permute-start.1 = (f32[1024,128]{1,0:T(8,128)}, f32[1024,128]{1,0:T(8,128)S(1)}, u32[]{:S(2)}, u32[]{:S(2)}) collective-permute-start(f32[1024,128]{1,0:T(8,128)} %refs_2_.3), channel_id=1, source_target_pairs={{0,4},{4,0},{1,5},{5,1},{2,6},{6,2},{3,7},{7,3},{8,12},{12,8},{9,1... | collective-permute-start | bytes 1572872 | tf_op jit(solution)/shard_map/ppermute | solution.py:175
  5.0 16.2 %copy-start.6 = (f32[1024,128]{1,0:T(8,128)S(1)}, f32[1024,128]{1,0:T(8,128)}, u32[]{:S(2)}) copy-start(f32[1024,128]{1,0:T(8,128)} %param.23) | copy-start | bytes 1572868
  27.1 0.8 %copy-start.9 = (f32[1024,128]{1,0:T(8,128)}, f32[1024,128]{1,0:T(8,128)S(1)}, u32[]{:S(2)}) copy-start(f32[1024,128]{1,0:T(8,128)S(1)} %collective-permute-done.1.refs_3_) | copy-start | bytes 1572868
  32.7 2.3 %copy-start.2 = (f32[1024,256]{1,0:T(8,128)S(1)}, f32[1024,256]{1,0:T(8,128)}, u32[]{:S(2)}) copy-start(f32[1024,256]{1,0:T(8,128)} %get-tuple-element.24) | copy-start | bytes 3145732
  35.0 1.2 %copy-start.1 = (f32[1024,256]{1,0:T(8,128)S(1)}, f32[1024,256]{1,0:T(8,128)}, u32[]{:S(2)}) copy-start(f32[1024,256]{1,0:T(8,128)} %get-tuple-element.21.refs_4_) | copy-start | bytes 3145732
  35.0 1.3 %copy-start.8 = (f32[1024,128]{1,0:T(8,128)S(1)}, f32[1024,128]{1,0:T(8,128)}, u32[]{:S(2)}) copy-start(f32[1024,128]{1,0:T(8,128)} %param.22) | copy-start | bytes 1572868
  37.4 1.9 %collective-permute-start.4 = (f32[384,128]{1,0:T(8,128)S(1)}, f32[384,128]{1,0:T(8,128)S(1)}, u32[]{:S(2)}, u32[]{:S(2)}) collective-permute-start(f32[384,128]{1,0:T(8,128)S(1)} %dynamic-slice_bitcast_fusion), channel_id=1, source_target_pairs={{0,8},{8,0},{16,24},{24,16},{1,9},{9,1},{17,25},{25,17},{2,10},{10... | collective-permute-start | bytes 589832 | tf_op jit(solution)/shard_map/ppermute | solution.py:175
  38.6 2.6 %copy-start.3 = (f32[256,512]{1,0:T(8,128)S(1)}, f32[256,512]{1,0:T(8,128)}, u32[]{:S(2)}) copy-start(f32[256,512]{1,0:T(8,128)} %param.19) | copy-start | bytes 1572868
  38.8 13.6 %collective-permute-start.2 = (f32[2,2,64,512]{3,2,1,0:T(8,128)S(1)}, f32[2,2,64,512]{3,2,1,0:T(8,128)S(1)}, u32[]{:S(2)}, u32[]{:S(2)}) collective-permute-start(f32[2,2,64,512]{3,2,1,0:T(8,128)S(1)} %bitcast.50), channel_id=1, source_target_pairs={{0,8},{8,0},{16,24},{24,16},{1,9},{9,1},{17,25},{25,17},{2,10},{10... | collective-permute-start | bytes 1572872 | tf_op jit(solution)/shard_map/ppermute | solution.py:175
  39.4 8.8 %copy-start.4 = (f32[256,512]{1,0:T(8,128)S(1)}, f32[256,512]{1,0:T(8,128)}, u32[]{:S(2)}) copy-start(f32[256,512]{1,0:T(8,128)} %param.20) | copy-start | bytes 1572868
  39.4 8.8 %copy-start.7 = (f32[1024,512]{1,0:T(8,128)S(1)}, f32[1024,512]{1,0:T(8,128)}, u32[]{:S(2)}) copy-start(f32[1024,512]{1,0:T(8,128)} %param.29) | copy-start | bytes 6291460
  39.4 6.9 %collective-permute-start.5 = (f32[384,128]{1,0:T(8,128)S(1)}, f32[384,128]{1,0:T(8,128)S(1)}, u32[]{:S(2)}, u32[]{:S(2)}) collective-permute-start(f32[384,128]{1,0:T(8,128)S(1)} %bitcast_add_fusion.1), channel_id=1, source_target_pairs={{0,16},{8,24},{16,0},{24,8},{1,17},{9,25},{17,1},{25,9},{2,18},{10... | collective-permute-start | bytes 589832 | tf_op jit(solution)/shard_map/ppermute | solution.py:175
  46.3 4.4 %copy-start.10 = (f32[384,128]{1,0:T(8,128)}, f32[384,128]{1,0:T(8,128)S(1)}, u32[]{:S(2)}) copy-start(f32[384,128]{1,0:T(8,128)S(1)} %add.57.rest_0_) | copy-start | bytes 589828
  46.3 6.0 %collective-permute-start.6 = (f32[384,128]{1,0:T(8,128)S(1)}, f32[384,128]{1,0:T(8,128)S(1)}, u32[]{:S(2)}, u32[]{:S(2)}) collective-permute-start(f32[384,128]{1,0:T(8,128)S(1)} %add.57.rest_0_), channel_id=1, source_target_pairs={{0,4},{4,0},{1,5},{5,1},{2,6},{6,2},{3,7},{7,3},{8,12},{12,8},{9,1... | collective-permute-start | bytes 589832 | tf_op jit(solution)/shard_map/ppermute | solution.py:175
  50.7 4.4 %collective-permute-start.7 = (f32[384,128]{1,0:T(8,128)S(1)}, f32[384,128]{1,0:T(8,128)S(1)}, u32[]{:S(2)}, u32[]{:S(2)}) collective-permute-start(f32[384,128]{1,0:T(8,128)S(1)} %add.57.rest_0_), channel_id=1, source_target_pairs={{0,8},{8,0},{16,24},{24,16},{1,9},{9,1},{17,25},{25,17},{2,10},{10... | collective-permute-start | bytes 589832 | tf_op jit(solution)/shard_map/ppermute | solution.py:175
  52.4 2.7 %copy-start.14 = (f32[384,128]{1,0:T(8,128)}, f32[384,128]{1,0:T(8,128)S(1)}, u32[]{:S(2)}) copy-start(f32[384,128]{1,0:T(8,128)S(1)} %collective-permute-done.6.rest_1_) | copy-start | bytes 589828
  52.4 3.4 %collective-permute-start.8 = (f32[384,128]{1,0:T(8,128)S(1)}, f32[384,128]{1,0:T(8,128)}, u32[]{:S(2)}, u32[]{:S(2)}) collective-permute-start(f32[384,128]{1,0:T(8,128)S(1)} %collective-permute-done.6.rest_1_), channel_id=1, source_target_pairs={{0,8},{8,0},{16,24},{24,16},{1,9},{9,1},{17,25},{25,17},{2,10},{10... | collective-permute-start | bytes 589832 | tf_op jit(solution)/shard_map/ppermute | solution.py:175
  52.5 0.8 %copy-start.5 = (f32[2,2,64,512]{3,2,1,0:T(8,128)}, f32[2,2,64,512]{3,2,1,0:T(8,128)S(1)}, u32[]{:S(2)}) copy-start(f32[2,2,64,512]{3,2,1,0:T(8,128)S(1)} %bitcast_add_fusion) | copy-start | bytes 1572868
  53.3 12.1 %collective-permute-start.3 = (f32[1,2,64,512]{3,2,1,0:T(8,128)S(1)}, f32[1,2,64,512]{3,2,1,0:T(8,128)}, u32[]{:S(2)}, u32[]{:S(2)}) collective-permute-start(f32[1,2,64,512]{3,2,1,0:T(8,128)S(1)} %constant_dynamic-slice_fusion), channel_id=1, source_target_pairs={{0,16},{8,24},{16,0},{24,8},{1,17},{9,25},{17,1},{25,9},{2,18},{10... | collective-permute-start | bytes 786440 | tf_op jit(solution)/shard_map/ppermute | solution.py:175
  63.1 3.4 %copy-start.11 = (f32[256,256]{1,0:T(8,128)S(1)}, f32[256,256]{1,0:T(8,128)}, u32[]{:S(2)}) copy-start(f32[256,256]{1,0:T(8,128)} %get-tuple-element.17) | copy-start | bytes 786436
  63.1 3.4 %copy-start.12 = (f32[64,512]{1,0:T(8,128)S(1)}, f32[64,512]{1,0:T(8,128)}, u32[]{:S(2)}) copy-start(f32[64,512]{1,0:T(8,128)} %param.28) | copy-start | bytes 393220
  63.1 4.4 %copy-start.13 = (f32[64,512]{1,0:T(8,128)S(1)}, f32[64,512]{1,0:T(8,128)}, u32[]{:S(2)}) copy-start(f32[64,512]{1,0:T(8,128)} %param.27) | copy-start | bytes 393220
  (1 other events, 0.7 us)
